TPU v7x, 32 devices: a whole 2x2x4 slice. The times are simulated.
32 devices in a mesh: node: 32 (over z, y, x, core).
Axes of the slice: x: 2, y: 2, z: 4, core: 2. Of those that a mesh axis runs over, the one named last changes fastest.
Arguments:
- labels: bfloat16 [131072, 512], P('node'), may hold values from -6 to 6
- seed_mask: int32 [131072], P('node'), may hold values 0 or 1
- band_w: bfloat16 [1024, 3, 128, 128], P('node'), may hold values from 0.0009994507 to 1
- far_block: int32 [32, 32, 2], P('node'), may hold values from 0 to 511
- far_tile: int32 [32, 32, 2], P('node'), may hold values from 0 to 31
- far_count: int32 [32, 32], P('node'), may hold values from 0 to 2, as said below
- far_w: bfloat16 [32, 32, 2, 8, 128], P('node'), may hold values from 0.049804688 to 2
Outputs:
- final_labels: bfloat16 [131072, 512], P('node')
- residual: float32 [2, 1024], P(None, 'node')
Inputs may be any that keep to these rules, and one draw needn't show every extreme that they name: `far_count`: in every draw at least one destination shard has all 2 slots live from every source shard; other counts vary from pair to pair.
All inputs are finite; a program needn't handle non-finite values. No bound on the sum of `seed_mask` on one device may be relied on, other than what follows from the above.
Results may differ from a plain program's by a relative error of at most 0.0027.
Values may be sent and summed in bfloat16 or wider, within the bound.
A program may use at most 128 MiB of HBM per device.

v0:
```python
import jax
import jax.numpy as jnp
from jax import lax
from jax.sharding import PartitionSpec as P

ITERS = 2


def with_halo(block, sides, width):
    for axis, dim in sides:
        count = lax.axis_size(axis)
        forward = [(i, i + 1) for i in range(count - 1)]
        forward.append((count - 1, 0))
        backward = [(target, source) for source, target in forward]
        low = lax.ppermute(
            lax.slice_in_dim(block, block.shape[dim] - width, None, axis=dim), axis, forward
        )
        high = lax.ppermute(lax.slice_in_dim(block, 0, width, axis=dim), axis, backward)
        block = jnp.concatenate([low, block, high], axis=dim)
    return block


def fetch_blocks(current, requests, block_rows, classes):
    blocks = current.reshape(-1, block_rows, classes)[requests]
    return lax.all_to_all(blocks, "node", split_axis=0, concat_axis=0, tiled=True)


def cycle_tiles(current, tile_count, tile_rows, classes):
    tiles = current.reshape(tile_count, tile_rows, classes)
    return with_halo(tiles, (("node", 0),), 1)


def body(labels, seed_mask, band_w, far_block, far_tile, far_count, far_w):
    node_rows, classes = labels.shape
    tile_count = band_w.shape[0]
    tile_rows = band_w.shape[2]
    peer_count = far_w.shape[1]
    slot_count = far_w.shape[2]
    block_rows = far_w.shape[3]
    requests = lax.all_to_all(far_block, "node", split_axis=1, concat_axis=0, tiled=True).reshape(
        peer_count, slot_count
    )
    live_slots = jnp.arange(slot_count)[None, :] < far_count[0][:, None]
    weights = jnp.where(live_slots[:, :, None, None], far_w[0], jnp.zeros((), jnp.bfloat16))
    flat_tiles = far_tile[0].reshape(-1)
    weight_sums = jnp.sum(weights, axis=2, dtype=jnp.float32).reshape(-1, tile_rows)
    degree_far = jnp.zeros((tile_count, tile_rows), jnp.float32).at[flat_tiles].add(weight_sums)
    degree = jnp.sum(band_w, axis=(1, 3), dtype=jnp.float32) + degree_far
    slot_weights = weights.reshape(peer_count * slot_count, block_rows, tile_rows)
    onehot = jnp.arange(tile_count)[:, None] == flat_tiles[None, :]
    placed = jnp.where(onehot[:, :, None, None], slot_weights[None], jnp.zeros((), jnp.bfloat16))
    placed = placed.reshape(tile_count, peer_count * slot_count * block_rows, tile_rows)
    seeded = (seed_mask == 1).reshape(tile_count, tile_rows, 1)
    clamped = labels.astype(jnp.float32).reshape(tile_count, tile_rows, classes)
    current = labels
    residuals = []
    for sweep in range(ITERS):
        padded = cycle_tiles(current, tile_count, tile_rows, classes)
        received = fetch_blocks(current, requests, block_rows, classes)
        band_sum = jnp.zeros((tile_count, tile_rows, classes), jnp.float32)
        for offset in (-1, 0, 1):
            source = padded[1 + offset : 1 + offset + tile_count]
            band_sum = band_sum + jnp.einsum(
                "itr,irc->itc", band_w[:, offset + 1], source, preferred_element_type=jnp.float32
            )
        far_sum = jnp.einsum(
            "tqr,qc->trc", placed, received.reshape(-1, classes), preferred_element_type=jnp.float32
        )
        averaged = (band_sum + far_sum) / degree[:, :, None]
        row_scale = jnp.sqrt(jnp.mean(averaged * averaged, axis=2, keepdims=True))
        scaled = averaged / jnp.maximum(row_scale, 0.05)
        fresh = jnp.where(seeded, clamped, scaled).astype(jnp.bfloat16)
        previous = current.astype(jnp.float32).reshape(tile_count, tile_rows, classes)
        residuals.append(jnp.sum(jnp.abs(fresh.astype(jnp.float32) - previous), axis=(1, 2)))
        current = fresh.reshape(node_rows, classes)
    return (current, jnp.stack(residuals))


def solution(mesh):
    placed = (
        P("node", None),
        P("node"),
        P("node", None, None, None),
        P("node", None, None),
        P("node", None, None),
        P("node", None),
        P("node", None, None, None, None),
    )
    return jax.shard_map(
        body,
        mesh=mesh,
        in_specs=placed,
        out_specs=(P("node", None), P(None, "node")),
        check_vma=False,
    )
```

profile of v0, /device:TPU:0, one launch (start us, length us, event | category | flops | bytes accessed | tf_op | source)
XLA Modules:
  0.0 134.0 jit_solution(6983224722722546354)
XLA Ops:
  0.6 0.0 copy-start.6
  0.6 0.0 copy-start.8
  0.7 1.5 %copy.30 = s32[1,32,2]{2,0,1:T(1,128)} copy(s32[1,32,2]{1,2,0:T(2,128)} %param.10) | data formatting | bytes 512 | tf_op args[3]
  2.2 7.5 %all-to-all-start = ((s32[1,32,2]{2,0,1:T(1,128)}), s32[1,32,2]{2,0,1:T(1,128)}, u32[]{:S(2)}, u32[]{:S(2)}) async-start(s32[1,32,2]{2,0,1:T(1,128)} %copy.30), calls=%async_computation | async-start | bytes 32768 | tf_op jit(solution)/shard_map/all_to_all | solution.py:40
  9.6 1.7 %slice_bitcast_fusion = (bf16[1,128,512]{2,1,0:T(8,128)(2,1)}, bf16[1,128,512]{2,1,0:T(8,128)(2,1)}) fusion(bf16[4096,512]{1,0:T(8,128)(2,1)} %param.7), kind=kLoop, calls=%fused_computation.59 | loop fusion | bytes 524288 | tf_op jit(solution)/shard_map/slice | solution.py:18
  11.4 5.1 %collective-permute-start.1 = (bf16[1,128,512]{2,1,0:T(8,128)(2,1)}, bf16[1,128,512]{2,1,0:T(8,128)(2,1)}, u32[]{:S(2)}, u32[]{:S(2)}) collective-permute-start(bf16[1,128,512]{2,1,0:T(8,128)(2,1)} %get-tuple-element.6), channel_id=1, source_target_pairs={{1,0},{2,1},{3,2},{4,3},{5,4},{6,5},{7,6},{8,7},{9,8},{10,9},{11,1... | collective-permute-start | bytes 393224 | tf_op jit(solution)/shard_map/ppermute | solution.py:18
  16.5 0.0 collective-permute-start
  16.5 0.8 copy.27
  17.2 0.1 reshape_squeeze.3
  17.3 0.1 eq.28
  17.5 0.7 iota_compare_fusion.1
  18.2 0.1 lt.51
  18.3 0.1 broadcast_in_dim.74
  18.4 0.1 broadcast_in_dim.75
  18.5 0.5 fusion.39
  19.0 0.1 iota_compare_fusion
  19.1 2.5 %convert_reduce_fusion = f32[32,128]{1,0:T(8,128)S(1)} fusion(bf16[32,3,128,128]{3,2,1,0:T(8,128)(2,1)} %param.9), kind=kLoop, calls=%fused_computation.19 | loop fusion | flops 3141632 | bytes 3162112 | tf_op jit(solution)/shard_map/reduce_sum | solution.py:48
  21.6 1.0 bitcast_select_fusion.1
  22.7 0.0 copy-done.8
  22.7 0.8 convert_reduce_fusion.1
  23.5 0.1 copy.28
  23.6 0.0 copy-start.9
  23.6 0.1 copy.29
  23.7 1.1 scatter_fusion
  24.9 0.0 all-to-all-done
  24.9 0.8 copy.31
  25.7 0.1 copy.32
  25.8 0.1 reshape.183
  25.9 3.6 %gather_fusion = bf16[64,8,512]{2,1,0:T(8,128)(2,1)} fusion(bf16[512,8,512]{2,1,0:T(8,128)(2,1)} %bitcast.77, s32[1024]{0:T(1024)S(1)} %pad_clamp_fusion), kind=kCustom, calls=%fused_computation | custom fusion | bytes 1048832 | tf_op jit(solution)/shard_map/gather | solution.py:24
  29.5 5.8 %all-to-all-start.1 = ((bf16[32,2,8,512]{3,2,1,0:T(8,128)(2,1)}), bf16[32,2,8,512]{3,2,1,0:T(8,128)(2,1)}, u32[]{:S(2)}, u32[]{:S(2)}) async-start(bf16[32,2,8,512]{3,2,1,0:T(8,128)(2,1)} %bitcast.85), calls=%async_computation.1 | async-start | bytes 1048576 | tf_op jit(solution)/shard_map/all_to_all | solution.py:25
  35.3 0.0 copy-done.6
  35.3 0.0 copy-start.11
  35.4 0.0 copy-start
  35.4 6.8 %fusion.29 = f32[32,128,512]{2,1,0:T(8,128)} fusion(bf16[32,128,512]{2,1,0:T(8,128)(2,1)} %bitcast.78, bf16[32,3,128,128]{3,2,1,0:T(8,128)(2,1)S(1)} %copy-done.6), kind=kOutput, calls=%fused_computation.46 | convolution fusion | flops 536870912 | bytes 13631488 | tf_op jit(solution)/shard_map/itr,irc->itc/dot_general | solution.py:63
  42.2 0.0 copy-done.11
  42.2 0.0 collective-permute-done
  42.2 0.0 copy-done
  42.2 5.4 %fusion.17 = f32[32,512,128]{1,2,0:T(8,128)} fusion(bf16[32,128,512]{2,1,0:T(8,128)(2,1)S(1)} %bitcast.79, bf16[1,128,512]{2,1,0:T(8,128)(2,1)} %collective-permute-done, bf16[32,3,128,128]{3,2,1,0:T(8,128)(2,1)S(1)} %copy-done.6), kind=kOutput, calls=%fused_computation.34 | convolution fusion | flops 545259520 | bytes 13762560 | tf_op jit(solution)/shard_map/itr,irc->itc/dot_general | solution.py:63
  47.6 3.3 %all-to-all-done.1 = bf16[32,2,8,512]{3,2,1,0:T(8,128)(2,1)} async-done(((bf16[32,2,8,512]{3,2,1,0:T(8,128)(2,1)}), bf16[32,2,8,512]{3,2,1,0:T(8,128)(2,1)}, u32[]{:S(2)}, u32[]{:S(2)}) %all-to-all-start.1) | async-done | bytes 524320 | tf_op jit(solution)/shard_map/all_to_all | solution.py:25
  50.9 6.8 %fusion.9 = f32[32,128,512]{2,1,0:T(8,128)} fusion(bf16[512,512,1]{1,0,2:T(8,128)(2,1)} %bitcast.16, pred[32,512]{1,0:T(8,128)(4,1)S(1)} %copy.28, bf16[512,128]{0,1:T(8,128)(2,1)S(1)} %copy.29), kind=kOutput, calls=%fused_computation.22 | convolution fusion | flops 2149580800 | bytes 9060352 | tf_op jit(solution)/shard_map/tqr,qc->trc/dot_general | solution.py:66
  57.7 0.0 collective-permute-done.1
  57.7 0.0 copy-done.1
  57.7 13.6 %multiply_reduce_fusion.1 = (f32[32,128]{1,0:T(8,128)S(1)}, f32[32,128,512]{2,1,0:T(8,128)}) fusion(f32[32,128]{1,0:T(8,128)S(1)} %scatter_fusion, f32[32,128,512]{2,1,0:T(8,128)} %fusion.9, bf16[1,128,512]{2,1,0:T(8,128)(2,1)} %collective-permute-done.1, bf16[32,128,512]{2,1,0:T(8,128)(2,1)S(1)} %bitcast.80, bf16[32,3,128,128]{3,2,1,0:T(8,128)(2,1)S(1)} %copy-done.6, ...), kind=kOutput, calls=%fused_computation.18 | convolution fusion | flops 557838336 | bytes 38961152 | tf_op jit(solution)/shard_map/itr,irc->itc/dot_general | solution.py:63
  71.3 5.0 %fusion.2 = bf16[32,128,512]{2,1,0:T(8,128)(2,1)S(1)} fusion(f32[32,128,512]{2,1,0:T(8,128)} %get-tuple-element.9, f32[32,128]{1,0:T(8,128)S(1)} %maximum_multiply_fusion.1, pred[32,128]{1,0:T(8,128)(4,1)S(1)} %compare_bitcast_fusion, bf16[4096,512]{1,0:T(8,128)(2,1)S(1)} %copy-done.1), kind=kLoop, calls=%fused_computation.9 | loop fusion | flops 8388608 | bytes 16797696 | tf_op jit(solution)/shard_map/convert_element_type | solution.py:72
  76.3 0.0 copy-start.3
  76.3 2.0 %copy-done.3 = bf16[32,128,512]{2,1,0:T(8,128)(2,1)} copy-done((bf16[32,128,512]{2,1,0:T(8,128)(2,1)}, bf16[32,128,512]{2,1,0:T(8,128)(2,1)S(1)}, u32[]{:S(2)}) %copy-start.3) | copy-done | bytes 4194328
  78.3 0.7 fusion.46
  79.0 0.0 collective-permute-start.2
  79.0 3.6 %gather_fusion.1 = bf16[64,8,512]{2,1,0:T(8,128)(2,1)} fusion(bf16[512,8,512]{2,1,0:T(8,128)(2,1)} %bitcast.82, s32[1024]{0:T(1024)S(1)} %pad_clamp_fusion), kind=kCustom, calls=%fused_computation.1 | custom fusion | bytes 1048832 | tf_op jit(solution)/shard_map/gather | solution.py:24
  82.6 5.8 %all-to-all-start.2 = ((bf16[32,2,8,512]{3,2,1,0:T(8,128)(2,1)}), bf16[32,2,8,512]{3,2,1,0:T(8,128)(2,1)}, u32[]{:S(2)}, u32[]{:S(2)}) async-start(bf16[32,2,8,512]{3,2,1,0:T(8,128)(2,1)} %bitcast.84), calls=%async_computation.2 | async-start | bytes 1048576 | tf_op jit(solution)/shard_map/all_to_all | solution.py:25
  88.4 0.0 copy-start.4
  88.4 6.8 %fusion.27 = f32[32,512,128]{1,2,0:T(8,128)} fusion(bf16[32,128,512]{2,1,0:T(8,128)(2,1)} %copy-done.3, bf16[32,3,128,128]{3,2,1,0:T(8,128)(2,1)S(1)} %copy-done.6), kind=kOutput, calls=%fused_computation.44 | convolution fusion | flops 536870912 | bytes 13631488 | tf_op jit(solution)/shard_map/itr,irc->itc/dot_general | solution.py:63
  95.2 5.1 %collective-permute-start.3 = (bf16[1,128,512]{2,1,0:T(8,128)(2,1)}, bf16[1,128,512]{2,1,0:T(8,128)(2,1)}, u32[]{:S(2)}, u32[]{:S(2)}) collective-permute-start(bf16[1,128,512]{2,1,0:T(8,128)(2,1)} %get-tuple-element.4), channel_id=1, source_target_pairs={{1,0},{2,1},{3,2},{4,3},{5,4},{6,5},{7,6},{8,7},{9,8},{10,9},{11,1... | collective-permute-start | bytes 393224 | tf_op jit(solution)/shard_map/ppermute | solution.py:18
  100.4 0.0 collective-permute-done.2
  100.4 4.5 %fusion.13 = f32[32,512,128]{1,2,0:T(8,128)} fusion(bf16[32,128,512]{2,1,0:T(8,128)(2,1)S(1)} %copy-done.4, bf16[1,128,512]{2,1,0:T(8,128)(2,1)S(1)} %collective-permute-done.2, bf16[32,3,128,128]{3,2,1,0:T(8,128)(2,1)S(1)} %copy-done.6), kind=kOutput, calls=%fused_computation.28 | convolution fusion | flops 545259520 | bytes 13762560 | tf_op jit(solution)/shard_map/itr,irc->itc/dot_general | solution.py:63
  104.8 0.0 all-to-all-done.2
  104.8 6.8 %fusion.7 = f32[32,128,512]{2,1,0:T(8,128)} fusion(bf16[512,512,1]{1,0,2:T(8,128)(2,1)} %bitcast.24, pred[32,512]{1,0:T(8,128)(4,1)S(1)} %copy-done.10, bf16[512,128]{0,1:T(8,128)(2,1)S(1)} %copy.29), kind=kOutput, calls=%fused_computation.20 | convolution fusion | flops 2149580800 | bytes 9060352 | tf_op jit(solution)/shard_map/tqr,qc->trc/dot_general | solution.py:66
  111.6 0.0 collective-permute-done.3
  111.6 13.7 %multiply_reduce_fusion = (f32[32,128]{1,0:T(8,128)S(1)}, f32[32,128,512]{2,1,0:T(8,128)}) fusion(f32[32,128]{1,0:T(8,128)S(1)} %scatter_fusion, f32[32,128,512]{2,1,0:T(8,128)} %fusion.7, bf16[1,128,512]{2,1,0:T(8,128)(2,1)} %collective-permute-done.3, bf16[32,128,512]{2,1,0:T(8,128)(2,1)S(1)} %copy-done.5, bf16[32,3,128,128]{3,2,1,0:T(8,128)(2,1)} %param.9, ...), kind=kOutput, calls=%fused_computation.17 | convolution fusion | flops 557838336 | bytes 38961152 | tf_op jit(solution)/shard_map/itr,irc->itc/dot_general | solution.py:63
  125.4 0.0 copy-done.2
  125.4 5.0 %fusion.3 = bf16[32,128,512]{2,1,0:T(8,128)(2,1)S(1)} fusion(f32[32,128,512]{2,1,0:T(8,128)} %get-tuple-element.11, f32[32,128]{1,0:T(8,128)S(1)} %maximum_multiply_fusion, pred[32,128]{1,0:T(8,128)(4,1)S(1)} %compare_bitcast_fusion, bf16[4096,512]{1,0:T(8,128)(2,1)S(1)} %copy-done.2), kind=kLoop, calls=%fused_computation.10 | loop fusion | flops 8388608 | bytes 16797696 | tf_op jit(solution)/shard_map/convert_element_type | solution.py:72
  130.4 0.0 copy-start.7
  130.4 3.1 %fusion.5 = (f32[32]{0:T(128)S(1)}, f32[32]{0:T(128)S(1)}) fusion(bf16[32,128,512]{2,1,0:T(8,128)(2,1)S(1)} %bitcast.81, bf16[32,128,512]{2,1,0:T(8,128)(2,1)S(1)} %copy-done.5, bf16[32,128,512]{2,1,0:T(8,128)(2,1)S(1)} %fusion.3), kind=kLoop, calls=%fused_computation.12 | loop fusion | flops 18874304 | bytes 12583168 | tf_op jit(solution)/shard_map/reduce_sum | solution.py:74
  133.4 0.6 pad_maximum_fusion.12
  (15 shorter events, 0.1 us)
Async XLA Ops:
  0.6 34.7 %copy-start.6 = (bf16[32,3,128,128]{3,2,1,0:T(8,128)(2,1)S(1)}, bf16[32,3,128,128]{3,2,1,0:T(8,128)(2,1)}, u32[]{:S(2)}) copy-start(bf16[32,3,128,128]{3,2,1,0:T(8,128)(2,1)} %param.9) | copy-start | bytes 9437188
  0.6 22.0 %copy-start.8 = (bf16[1,32,2,8,128]{4,3,2,1,0:T(8,128)(2,1)S(1)}, bf16[1,32,2,8,128]{4,3,2,1,0:T(8,128)(2,1)}, u32[]{:S(2)}) copy-start(bf16[1,32,2,8,128]{4,3,2,1,0:T(8,128)(2,1)} %param.13) | copy-start | bytes 393220
  2.2 22.7 %all-to-all-start = ((s32[1,32,2]{2,0,1:T(1,128)}), s32[1,32,2]{2,0,1:T(1,128)}, u32[]{:S(2)}, u32[]{:S(2)}) async-start(s32[1,32,2]{2,0,1:T(1,128)} %copy.30), calls=%async_computation | async-start | bytes 32768 | tf_op jit(solution)/shard_map/all_to_all | solution.py:40
  11.4 46.3 %collective-permute-start.1 = (bf16[1,128,512]{2,1,0:T(8,128)(2,1)}, bf16[1,128,512]{2,1,0:T(8,128)(2,1)}, u32[]{:S(2)}, u32[]{:S(2)}) collective-permute-start(bf16[1,128,512]{2,1,0:T(8,128)(2,1)} %get-tuple-element.6), channel_id=1, source_target_pairs={{1,0},{2,1},{3,2},{4,3},{5,4},{6,5},{7,6},{8,7},{9,8},{10,9},{11,1... | collective-permute-start | bytes 393224 | tf_op jit(solution)/shard_map/ppermute | solution.py:18
  16.5 25.7 %collective-permute-start = (bf16[1,128,512]{2,1,0:T(8,128)(2,1)}, bf16[1,128,512]{2,1,0:T(8,128)(2,1)}, u32[]{:S(2)}, u32[]{:S(2)}) collective-permute-start(bf16[1,128,512]{2,1,0:T(8,128)(2,1)} %get-tuple-element.7), channel_id=1, source_target_pairs={{0,1},{1,2},{2,3},{3,4},{4,5},{5,6},{6,7},{7,8},{8,9},{9,10},{10,1... | collective-permute-start | bytes 393224 | tf_op jit(solution)/shard_map/ppermute | solution.py:15
  23.6 27.3 %copy-start.9 = (pred[32,512]{1,0:T(8,128)(4,1)}, pred[32,512]{1,0:T(8,128)(4,1)S(1)}, u32[]{:S(2)}) copy-start(pred[32,512]{1,0:T(8,128)(4,1)S(1)} %copy.28) | copy-start | bytes 49156
  29.5 21.4 %all-to-all-start.1 = ((bf16[32,2,8,512]{3,2,1,0:T(8,128)(2,1)}), bf16[32,2,8,512]{3,2,1,0:T(8,128)(2,1)}, u32[]{:S(2)}, u32[]{:S(2)}) async-start(bf16[32,2,8,512]{3,2,1,0:T(8,128)(2,1)} %bitcast.85), calls=%async_computation.1 | async-start | bytes 1048576 | tf_op jit(solution)/shard_map/all_to_all | solution.py:25
  35.3 6.8 %copy-start.11 = (s32[4096]{0:T(1024)S(1)}, s32[4096]{0:T(1024)}, u32[]{:S(2)}) copy-start(s32[4096]{0:T(1024)} %param.8) | copy-start | bytes 49156
  35.4 6.8 %copy-start = (bf16[4096,512]{1,0:T(8,128)(2,1)S(1)}, bf16[4096,512]{1,0:T(8,128)(2,1)}, u32[]{:S(2)}) copy-start(bf16[4096,512]{1,0:T(8,128)(2,1)} %param.7) | copy-start | bytes 12582916
  50.9 6.8 %copy-start.1 = (bf16[4096,512]{1,0:T(8,128)(2,1)S(1)}, bf16[4096,512]{1,0:T(8,128)(2,1)}, u32[]{:S(2)}) copy-start(bf16[4096,512]{1,0:T(8,128)(2,1)} %param.7) | copy-start | bytes 12582916
  76.3 2.0 %copy-start.3 = (bf16[32,128,512]{2,1,0:T(8,128)(2,1)}, bf16[32,128,512]{2,1,0:T(8,128)(2,1)S(1)}, u32[]{:S(2)}) copy-start(bf16[32,128,512]{2,1,0:T(8,128)(2,1)S(1)} %fusion.2) | copy-start | bytes 12582916
  79.0 21.4 %collective-permute-start.2 = (bf16[1,128,512]{2,1,0:T(8,128)(2,1)}, bf16[1,128,512]{2,1,0:T(8,128)(2,1)S(1)}, u32[]{:S(2)}, u32[]{:S(2)}) collective-permute-start(bf16[1,128,512]{2,1,0:T(8,128)(2,1)} %get-tuple-element.5), channel_id=1, source_target_pairs={{0,1},{1,2},{2,3},{3,4},{4,5},{5,6},{6,7},{7,8},{8,9},{9,10},{10,1... | collective-permute-start | bytes 393224 | tf_op jit(solution)/shard_map/ppermute | solution.py:15
  82.6 22.3 %all-to-all-start.2 = ((bf16[32,2,8,512]{3,2,1,0:T(8,128)(2,1)}), bf16[32,2,8,512]{3,2,1,0:T(8,128)(2,1)}, u32[]{:S(2)}, u32[]{:S(2)}) async-start(bf16[32,2,8,512]{3,2,1,0:T(8,128)(2,1)} %bitcast.84), calls=%async_computation.2 | async-start | bytes 1048576 | tf_op jit(solution)/shard_map/all_to_all | solution.py:25
  88.4 11.9 %copy-start.4 = (bf16[32,128,512]{2,1,0:T(8,128)(2,1)S(1)}, bf16[32,128,512]{2,1,0:T(8,128)(2,1)}, u32[]{:S(2)}) copy-start(bf16[32,128,512]{2,1,0:T(8,128)(2,1)} %copy-done.3) | copy-start | bytes 12582916
  95.2 9.6 %copy-start.10 = (pred[32,512]{1,0:T(8,128)(4,1)S(1)}, pred[32,512]{1,0:T(8,128)(4,1)}, u32[]{:S(2)}) copy-start(pred[32,512]{1,0:T(8,128)(4,1)} %copy-done.9) | copy-start | bytes 49156
  95.2 16.4 %collective-permute-start.3 = (bf16[1,128,512]{2,1,0:T(8,128)(2,1)}, bf16[1,128,512]{2,1,0:T(8,128)(2,1)}, u32[]{:S(2)}, u32[]{:S(2)}) collective-permute-start(bf16[1,128,512]{2,1,0:T(8,128)(2,1)} %get-tuple-element.4), channel_id=1, source_target_pairs={{1,0},{2,1},{3,2},{4,3},{5,4},{6,5},{7,6},{8,7},{9,8},{10,9},{11,1... | collective-permute-start | bytes 393224 | tf_op jit(solution)/shard_map/ppermute | solution.py:18
  104.8 6.8 %copy-start.5 = (bf16[32,128,512]{2,1,0:T(8,128)(2,1)S(1)}, bf16[32,128,512]{2,1,0:T(8,128)(2,1)}, u32[]{:S(2)}) copy-start(bf16[32,128,512]{2,1,0:T(8,128)(2,1)} %copy-done.3) | copy-start | bytes 12582916
  111.6 13.8 %copy-start.2 = (bf16[4096,512]{1,0:T(8,128)(2,1)S(1)}, bf16[4096,512]{1,0:T(8,128)(2,1)}, u32[]{:S(2)}) copy-start(bf16[4096,512]{1,0:T(8,128)(2,1)} %param.7) | copy-start | bytes 12582916
  130.4 3.1 %copy-start.7 = (bf16[32,128,512]{2,1,0:T(8,128)(2,1)}, bf16[32,128,512]{2,1,0:T(8,128)(2,1)S(1)}, u32[]{:S(2)}) copy-start(bf16[32,128,512]{2,1,0:T(8,128)(2,1)S(1)} %fusion.3) | copy-start | bytes 12582916
where the time goes:
time: 135 us; the launch traced here: 134 us
  matrix products  64.3 us (48%)
  starting transfers between devices  29.4 us (22%)
  other arithmetic  20.4 us (15%)
  local copies, waits for them, and re-layouts  15.7 us (12%)
  waiting for transfers between devices  3.36 us (2%)
    dot_general x6, matrix products, body(): jnp.einsum('itr,irc->itc', band_w[:, offset + 1], source, preferred_eleme...  50.8 us
    dot_general x2, matrix products, body(): jnp.einsum('tqr,qc->trc', placed, received.reshape(-1, classes), preferre...  13.5 us
    all_to_all x2, starting transfers between devices, fetch_blocks(): lax.all_to_all(blocks, 'node', split_axis=0, concat_axis=0, tiled=True)  11.7 us
    ppermute x2, starting transfers between devices, with_halo(): lax.ppermute(lax.slice_in_dim(block, 0, width, axis=dim), axis, backward)  10.2 us
    convert_element_type x2, other arithmetic, body(): fresh = jnp.where(seeded, clamped, scaled).astype(jnp.bfloat16)  9.95 us
    all_to_all x1, starting transfers between devices, body(): lax.all_to_all(far_block, 'node', split_axis=1, concat_axis=0, tiled=True)  7.45 us
    gather x2, local copies, waits for them, and re-layouts, fetch_blocks(): blocks = current.reshape(-1, block_rows, classes)[requests]  7.15 us
    unnamed x26, local copies, waits for them, and re-layouts  4.35 us
  transfers between devices with their start and end apart: 7, of which 1 were waited for; matrix products, arithmetic and copies ran while one was open for 41% of the time, Pallas kernels for 0%

commit v1 on v0

v1 whole, which is shorter than its diff:
```python
import functools

import jax
import jax.numpy as jnp
from jax import lax
from jax.experimental import pallas as pl
from jax.experimental.pallas import tpu as pltpu
from jax.sharding import PartitionSpec as P

ITERS = 2
MESH = pl.DeviceIdType.MESH
ROWS = 32
GROUP = 16


def kernel(
    dims,
    labels_hbm, band_hbm, farw_hbm, req_ref, slot_ref, seed_ref,
    out_hbm, res_ref,
    cur0, cur1, band, farw, wide_t, onehot, placed, acc, inv, part,
    halo0, halo1, send0, send1, recv0, recv1, req_in, req_s,
    lab_sem, band_sem, farw_sem, smem_sem, out_sem,
    req_send, req_recv, halo_send, halo_recv, blk_send, blk_recv,
):
    n, tiles, tile, slots, blk, classes = dims
    rows = tiles * tile
    lane = 128
    per = slots * blk
    far_rows = n * per
    me = lax.axis_index("node")
    right, left = lax.rem(me + 1, n), lax.rem(me + n - 1, n)
    cur = (cur0, cur1)
    halo, send, recv = (halo0, halo1), (send0, send1), (recv0, recv1)

    def groups(start, size):
        return pl.ds(start // GROUP, size // GROUP)

    def as_rows(value):
        return value.reshape(-1, classes)

    lab_copy = pltpu.make_async_copy(labels_hbm, cur0.at[groups(tile, rows)], lab_sem)
    band_copy = pltpu.make_async_copy(band_hbm, band, band_sem)
    farw_copy = pltpu.make_async_copy(farw_hbm, farw, farw_sem)
    lab_copy.start()
    farw_copy.start()
    band_copy.start()

    barrier = pltpu.get_barrier_semaphore()

    @pl.loop(1, n)
    def _(j):
        pl.semaphore_signal(barrier, inc=1, device_id=(lax.rem(me + j, n),), device_id_type=MESH)

    pl.semaphore_wait(barrier, n - 1)

    @pl.loop(1, n)
    def _(j):
        peer = lax.rem(me + j, n)
        pltpu.make_async_remote_copy(
            req_ref.at[peer], req_in.at[me], req_send, req_recv,
            device_id=(peer,), device_id_type=MESH,
        ).start()

    def halo_copies(it, low, high):
        return (
            pltpu.make_async_remote_copy(
                high, halo[it].at[0], halo_send.at[it, 0], halo_recv.at[it, 0],
                device_id=(right,), device_id_type=MESH,
            ),
            pltpu.make_async_remote_copy(
                low, halo[it].at[1], halo_send.at[it, 1], halo_recv.at[it, 1],
                device_id=(left,), device_id_type=MESH,
            ),
        )

    halo_first = halo_copies(
        0, labels_hbm.at[groups(0, tile)], labels_hbm.at[groups(rows - tile, tile)]
    )
    for copy in halo_first:
        copy.start()

    req_in[me] = req_ref[me]
    lab_copy.wait()
    pltpu.make_async_copy(req_in.at[pl.ds(0, n - 1)], req_in.at[pl.ds(0, n - 1)], req_recv).wait()
    smem_copy = pltpu.make_async_copy(req_in, req_s, smem_sem)
    smem_copy.start()
    smem_copy.wait()

    def block_copy(it, j):
        peer = lax.rem(me + j, n)
        return pltpu.make_async_remote_copy(
            send[it].at[peer], recv[it].at[me], blk_send.at[it], blk_recv.at[it],
            device_id=(peer,), device_id_type=MESH,
        )

    def gathered(it, peer):
        halves = []
        for k in range(slots):
            wanted = req_s[peer, 0, k]
            pair = cur[it][wanted // 2 + tile // GROUP].astype(jnp.float32)
            odd = jnp.full((blk, classes), wanted % 2, jnp.int32) == 1
            halves.append(jnp.where(odd, pair[blk:], pair[:blk]))
        return jnp.concatenate(halves, axis=0).astype(jnp.bfloat16)

    def exchange(it):
        @pl.loop(1, n)
        def _(j):
            peer = lax.rem(me + j, n)
            send[it][peer] = gathered(it, peer)

            @pl.when(j > 1)
            def _():
                block_copy(it, j - 1).start()

        recv[it][me] = gathered(it, me)
        block_copy(it, n - 1).start()

    def await_halo(it, copies):
        for copy in copies:
            copy.wait()
        cur[it][groups(0, tile)] = halo[it][0]
        cur[it][groups(rows + tile, tile)] = halo[it][1]

    def await_blocks(it):
        both = pl.ds(0, n - 1)
        pltpu.make_async_copy(send[it].at[both], send[it].at[both], blk_send.at[it]).wait()
        pltpu.make_async_copy(recv[it].at[both], recv[it].at[both], blk_recv.at[it]).wait()

    def band_pass(it):
        zero = jnp.zeros((tile, tile), jnp.bfloat16)

        @pl.loop(0, tiles // 2)
        def _(p):
            first = [band[2 * p, o] for o in range(3)]
            second = [band[2 * p + 1, o] for o in range(3)]
            weights = jnp.concatenate(
                [jnp.concatenate(first + [zero], axis=1), jnp.concatenate([zero] + second, axis=1)],
                axis=0,
            )
            base = pl.multiple_of(p * (2 * tile), 2 * tile)
            acc[pl.ds(base, 2 * tile), :] = jnp.dot(
                weights,
                as_rows(cur[it][pl.ds(p * (2 * tile // GROUP), 4 * tile // GROUP)]),
                preferred_element_type=jnp.float32,
            )

    def far_pass(it, p):
        base = pl.multiple_of(p * (2 * tile), 2 * tile)
        acc[pl.ds(base, 2 * tile), :] += jnp.dot(
            placed[pl.ds(base, 2 * tile), :],
            recv[it][...].reshape(far_rows, classes),
            preferred_element_type=jnp.float32,
        )

    def finish(it, p):
        target = cur[1 - it]
        for half in range(2):
            total = jnp.zeros((8, lane), jnp.float32)
            for r in range(0, tile, ROWS):
                base = pl.multiple_of(p * (2 * tile) + half * tile + r, ROWS)
                here = pl.ds(base, ROWS)
                spread = [acc[here, c : c + lane] for c in range(0, classes, lane)]
                squares = spread[0] * spread[0]
                for s in spread[1:]:
                    squares = squares + s * s
                mean = jnp.sum(squares, axis=1, keepdims=True) * (1.0 / classes)
                signed = inv[here, :]
                size = jnp.abs(signed)
                factor = size / jnp.maximum(size * jnp.sqrt(mean), 0.05)
                keep = signed < 0.0
                padded = pl.ds(
                    p * (2 * tile // GROUP) + (half * tile + r + tile) // GROUP, ROWS // GROUP
                )
                for q, s in enumerate(spread):
                    where = slice(q * lane, (q + 1) * lane)
                    before = cur[it][padded, :, where].reshape(ROWS, lane).astype(jnp.float32)
                    fresh = jnp.where(keep, before, s * factor).astype(jnp.bfloat16)
                    target[padded, :, where] = fresh.reshape(ROWS // GROUP, GROUP, lane)
                    change = jnp.abs(fresh.astype(jnp.float32) - before)
                    for i in range(0, ROWS, 8):
                        total = total + change[i : i + 8]
            part[2 * p + half] = total

    def prepare():
        wide_t[...] = farw[...].astype(jnp.float32).T
        count = slot_ref.shape[1]
        chosen = slot_ref[...] == lax.broadcasted_iota(jnp.int32, (tiles, count), 0)
        slot_of = lax.shift_right_logical(
            lax.broadcasted_iota(jnp.int32, (count, far_rows), 1), blk.bit_length() - 1
        )
        spread = slot_of == lax.broadcasted_iota(jnp.int32, (count, far_rows), 0)
        onehot[...] = jnp.dot(
            chosen.astype(jnp.float32).astype(jnp.bfloat16),
            spread.astype(jnp.float32).astype(jnp.bfloat16),
            preferred_element_type=jnp.float32,
        )

        @pl.loop(0, tiles)
        def _(t):
            base = pl.multiple_of(t * tile, tile)
            weights = wide_t[...] * onehot[pl.ds(t, 1), :]
            placed[pl.ds(base, tile), :] = weights.astype(jnp.bfloat16)
            total = band[t, 0].astype(jnp.float32)
            for o in range(1, 3):
                total = total + band[t, o].astype(jnp.float32)
            for c in range(0, far_rows, lane):
                total = total + weights[:, c : c + lane]
            degree = jnp.sum(total, axis=1, keepdims=True)
            seeded = jnp.broadcast_to(seed_ref[pl.ds(t, 1), :].astype(jnp.float32), (tile, tile)).T
            inverse = jnp.broadcast_to(1.0 / degree, (tile, tile))
            inv[pl.ds(base, tile), :] = jnp.where(seeded == 1.0, -inverse, inverse)

    def out_copy(p):
        base = p * (2 * tile // GROUP)
        return pltpu.make_async_copy(
            cur[ITERS % 2].at[pl.ds(base + tile // GROUP, 2 * tile // GROUP)],
            out_hbm.at[pl.ds(base, 2 * tile // GROUP)],
            out_sem,
        )

    for it in range(ITERS):
        if it:
            copies = halo_copies(
                it, cur[it].at[groups(tile, tile)], cur[it].at[groups(rows, tile)]
            )
        else:
            copies = halo_first
        exchange(it)
        if it:
            for copy in copies:
                copy.start()
        else:
            farw_copy.wait()
            band_copy.wait()
            prepare()
        await_halo(it, copies)
        band_pass(it)
        await_blocks(it)

        last = it == ITERS - 1

        @pl.loop(0, tiles // 2)
        def _(p):
            far_pass(it, p)
            finish(it, p)
            if last:

                @pl.when(p > 0)
                def _():
                    out_copy(p - 1).start()

        sums = jnp.sum(part[...], axis=1)
        res_ref[it : it + 1, :] = jnp.sum(sums.T, axis=0, keepdims=True)

    out_copy(tiles // 2 - 1).start()
    whole = pltpu.make_async_copy(cur[ITERS % 2].at[groups(tile, rows)], out_hbm, out_sem)
    whole.wait()
    both = pl.ds(0, n - 1)
    pltpu.make_async_copy(req_ref.at[both], req_ref.at[both], req_send).wait()


def body(labels, seed_mask, band_w, far_block, far_tile, far_count, far_w):
    rows, classes = labels.shape
    tiles, _, tile, _ = band_w.shape
    _, n, slots, blk, _ = far_w.shape
    lane = 128
    per = slots * blk
    live = jnp.arange(slots, dtype=jnp.int32)[None, :] < far_count[0][:, None]
    slot_tile = jnp.where(live, far_tile[0], -1).reshape(1, n * slots)
    requests = jnp.pad(far_block[0], ((0, 0), (0, lane - slots))).reshape(n, 1, lane)
    dims = (n, tiles, tile, slots, blk, classes)
    vmem, anywhere = pltpu.VMEM, pl.BlockSpec(memory_space=pl.ANY)
    held = pl.BlockSpec(memory_space=pltpu.VMEM)
    dma = pltpu.SemaphoreType.DMA
    bf16, f32 = jnp.bfloat16, jnp.float32
    out, residual = pl.pallas_call(
        functools.partial(kernel, dims),
        out_shape=(
            jax.ShapeDtypeStruct((rows // GROUP, GROUP, classes), bf16),
            jax.ShapeDtypeStruct((ITERS, tiles), f32),
        ),
        in_specs=[anywhere, anywhere, anywhere, held, held, held],
        out_specs=(anywhere, held),
        scratch_shapes=[
            vmem(((rows + 2 * tile) // GROUP, GROUP, classes), bf16),
            vmem(((rows + 2 * tile) // GROUP, GROUP, classes), bf16),
            vmem(band_w.shape, bf16),
            vmem((n * per, tile), bf16),
            vmem((tile, n * per), f32),
            vmem((tiles, n * per), f32),
            vmem((rows, n * per), bf16),
            vmem((rows, classes), f32),
            vmem((rows, lane), f32),
            vmem((tiles, 8, lane), f32),
            vmem((2, tile // GROUP, GROUP, classes), bf16),
            vmem((2, tile // GROUP, GROUP, classes), bf16),
            vmem((n, per, classes), bf16),
            vmem((n, per, classes), bf16),
            vmem((n, per, classes), bf16),
            vmem((n, per, classes), bf16),
            vmem((n, 1, lane), jnp.int32),
            pltpu.SMEM((n, 1, lane), jnp.int32),
            dma, dma, dma, dma, dma,
            dma, dma,
            dma((ITERS, 2)), dma((ITERS, 2)),
            dma((ITERS,)), dma((ITERS,)),
        ],
        compiler_params=pltpu.CompilerParams(
            collective_id=0, has_side_effects=True, vmem_limit_bytes=60 * 1024 * 1024
        ),
    )(
        labels.reshape(rows // GROUP, GROUP, classes),
        band_w,
        far_w.reshape(n * per, tile),
        requests,
        slot_tile,
        seed_mask.reshape(tiles, tile),
    )
    return out.reshape(rows, classes), residual


def solution(mesh):
    placed = (
        P("node", None),
        P("node"),
        P("node", None, None, None),
        P("node", None, None),
        P("node", None, None),
        P("node", None),
        P("node", None, None, None, None),
    )
    return jax.shard_map(
        body,
        mesh=mesh,
        in_specs=placed,
        out_specs=(P("node", None), P(None, "node")),
        check_vma=False,
    )
```

time: 135 us -> 74.5 us (0.55)
  Pallas kernels: 0 us -> 64.9 us
  matrix products: 64.3 us -> 0 us
  starting transfers between devices: 29.4 us -> 0 us
  other arithmetic: 20.4 us -> 1.25 us
  local copies, waits for them, and re-layouts: 15.7 us -> 7.39 us
  waiting for transfers between devices: 3.36 us -> 0 us
    pallas_call x0 -> x1, Pallas kernels: none -> 64.9 us  [body(): pl.pallas_call(functools.partial(kernel, dims), out_shape=(jax.ShapeDtype...]
    dot_general x8 -> x0, matrix products: 64.3 us -> none  [the longest x6 50.8 us: body(): jnp.einsum('itr,irc->itc', band_w[:, offset + 1], source, preferred_eleme...]
    all_to_all x3 -> x0, starting transfers between devices: 19.1 us -> none  [the longest x2 11.7 us: fetch_blocks(): lax.all_to_all(blocks, 'node', split_axis=0, concat_axis=0, tiled=True)]
    ppermute x4 -> x0, starting transfers between devices: 10.3 us -> none  [the longest x2 10.2 us: with_halo(): lax.ppermute(lax.slice_in_dim(block, 0, width, axis=dim), axis, backward)]
    convert_element_type x2 -> x0, other arithmetic: 9.95 us -> none  [body(): fresh = jnp.where(seeded, clamped, scaled).astype(jnp.bfloat16)]
    gather x2 -> x0, local copies, waits for them, and re-layouts: 7.15 us -> none  [fetch_blocks(): blocks = current.reshape(-1, block_rows, classes)[requests]]
    reduce_sum x3 -> x0, other arithmetic: 6.35 us -> none  [the longest x1 3.05 us: body(): jnp.sum(jnp.abs(fresh.astype(jnp.float32) - previous), axis=(1, 2))]
    all_to_all x3 -> x0, waiting for transfers between devices: 3.35 us -> none  [the longest x2 3.35 us: fetch_blocks(): lax.all_to_all(blocks, 'node', split_axis=0, concat_axis=0, tiled=True)]
  transfers between devices with their start and end apart: 7 -> 0, of which waited for: 1 -> 0; matrix products, arithmetic and copies ran while one was open for 41% -> 0% of each run, Pallas kernels for 0% -> 0%
where the time goes in v1:
time: 74.5 us; the launch traced here: 74.2 us
  Pallas kernels  64.9 us (87%)
  local copies, waits for them, and re-layouts  7.39 us (10%)
  other arithmetic  1.25 us (2%)
    pallas_call x1, Pallas kernels, body(): pl.pallas_call(functools.partial(kernel, dims), out_shape=(jax.ShapeDtype...  64.9 us
    unnamed x5, local copies, waits for them, and re-layouts  5.8 us

profile of v1, /device:TPU:0, one launch (start us, length us, event | category | flops | bytes accessed | tf_op | source)
XLA Modules:
  0.0 74.2 jit_solution(4438454401256640243)
XLA Ops:
  0.6 0.7 iota_compare_fusion
  1.4 0.1 lt.29
  1.5 0.8 %copy.11 = s32[32,2]{1,0:T(8,128)S(1)} copy(s32[32,2]{0,1:T(2,128)} %bitcast.12) | data formatting | bytes 512 | tf_op jit(solution)/shard_map/squeeze | solution.py:270
  2.2 0.6 pad.4
  2.8 0.8 %copy.12 = s32[1,32,2]{2,1,0:T(8,128)S(1)} copy(s32[1,32,2]{1,2,0:T(2,128)} %param.11) | data formatting | bytes 512 | tf_op args[4]
  3.6 0.1 squeeze.7
  3.7 0.5 broadcast_select_fusion.slot_ref
  4.2 64.9 %shard_map.86 = (bf16[256,16,512]{2,1,0:T(8,128)(2,1)}, f32[2,32]{1,0:T(2,128)}) custom-call(bf16[256,16,512]{2,1,0:T(8,128)(2,1)} %bitcast.7, bf16[32,3,128,128]{3,2,1,0:T(8,128)(2,1)} %band_hbm.1, bf16[512,128]{1,0:T(8,128)(2,1)} %bitcast.9, s32[32,1,128]{2,1,0:T(1,128)} %bitcast.10, s32[1,64]{1,0:T(1,128)} %broadcast_select_fusion.slot_ref, ...), custom_call_target="tpu_custom_call" | custom-call | tf_op jit(solution)/shard_map/pallas_call | solution.py:276
  69.2 0.0 copy-start
  69.2 4.5 %copy.15 = bf16[4096,512]{1,0:T(8,128)(2,1)} copy(bf16[4096,512]{1,0:T(8,128)(2,1)} %bitcast.8) | data formatting | bytes 8388608
  73.7 0.0 copy-done
  73.7 0.6 copy.16
Async XLA Ops:
  69.2 4.5 %copy-start = (f32[2,32]{1,0:T(2,128)S(1)}, f32[2,32]{1,0:T(2,128)}, u32[]{:S(2)}) copy-start(f32[2,32]{1,0:T(2,128)} %get-tuple-element.9) | copy-start | bytes 772

commit v2 on v1

--- a/solution.py
+++ b/solution.py
@@ -15,9 +15,9 @@
 
 def kernel(
     dims,
-    labels_hbm, band_hbm, farw_hbm, req_ref, slot_ref, seed_ref,
+    labels_hbm, band_hbm, farw_hbm, req_ref, tile_ref, count_ref, seed_ref,
     out_hbm, res_ref,
-    cur0, cur1, band, farw, wide_t, onehot, placed, acc, inv, part,
+    cur0, cur1, band, farw, wide_t, onehot, placed, acc, far_a, far_b, inv, part,
     halo0, halo1, send0, send1, recv0, recv1, req_in, req_s,
     lab_sem, band_sem, farw_sem, smem_sem, out_sem,
     req_send, req_recv, halo_send, halo_recv, blk_send, blk_recv,
@@ -57,7 +57,7 @@
     def _(j):
         peer = lax.rem(me + j, n)
         pltpu.make_async_remote_copy(
-            req_ref.at[peer], req_in.at[me], req_send, req_recv,
+            req_ref, req_in.at[me], req_send, req_recv,
             device_id=(peer,), device_id_type=MESH,
         ).start()
 
@@ -79,7 +79,7 @@
     for copy in halo_first:
         copy.start()
 
-    req_in[me] = req_ref[me]
+    req_in[me] = req_ref[...]
     lab_copy.wait()
     pltpu.make_async_copy(req_in.at[pl.ds(0, n - 1)], req_in.at[pl.ds(0, n - 1)], req_recv).wait()
     smem_copy = pltpu.make_async_copy(req_in, req_s, smem_sem)
@@ -96,7 +96,7 @@
     def gathered(it, peer):
         halves = []
         for k in range(slots):
-            wanted = req_s[peer, 0, k]
+            wanted = req_s[peer, k, me]
             pair = cur[it][wanted // 2 + tile // GROUP].astype(jnp.float32)
             odd = jnp.full((blk, classes), wanted % 2, jnp.int32) == 1
             halves.append(jnp.where(odd, pair[blk:], pair[:blk]))
@@ -126,10 +126,10 @@
         pltpu.make_async_copy(send[it].at[both], send[it].at[both], blk_send.at[it]).wait()
         pltpu.make_async_copy(recv[it].at[both], recv[it].at[both], blk_recv.at[it]).wait()
 
-    def band_pass(it):
+    def band_pass(it, start, stop):
         zero = jnp.zeros((tile, tile), jnp.bfloat16)
 
-        @pl.loop(0, tiles // 2)
+        @pl.loop(start, stop)
         def _(p):
             first = [band[2 * p, o] for o in range(3)]
             second = [band[2 * p + 1, o] for o in range(3)]
@@ -144,22 +144,26 @@
                 preferred_element_type=jnp.float32,
             )
 
-    def far_pass(it, p):
+    def far_pass(it, p, into):
         base = pl.multiple_of(p * (2 * tile), 2 * tile)
-        acc[pl.ds(base, 2 * tile), :] += jnp.dot(
+        into[...] = jnp.dot(
             placed[pl.ds(base, 2 * tile), :],
             recv[it][...].reshape(far_rows, classes),
             preferred_element_type=jnp.float32,
         )
 
-    def finish(it, p):
+    def finish(it, p, far):
         target = cur[1 - it]
         for half in range(2):
             total = jnp.zeros((8, lane), jnp.float32)
             for r in range(0, tile, ROWS):
                 base = pl.multiple_of(p * (2 * tile) + half * tile + r, ROWS)
                 here = pl.ds(base, ROWS)
-                spread = [acc[here, c : c + lane] for c in range(0, classes, lane)]
+                local = slice(half * tile + r, half * tile + r + ROWS)
+                spread = [
+                    acc[here, c : c + lane] + far[local, c : c + lane]
+                    for c in range(0, classes, lane)
+                ]
                 squares = spread[0] * spread[0]
                 for s in spread[1:]:
                     squares = squares + s * s
@@ -183,17 +187,22 @@
 
     def prepare():
         wide_t[...] = farw[...].astype(jnp.float32).T
-        count = slot_ref.shape[1]
-        chosen = slot_ref[...] == lax.broadcasted_iota(jnp.int32, (tiles, count), 0)
-        slot_of = lax.shift_right_logical(
-            lax.broadcasted_iota(jnp.int32, (count, far_rows), 1), blk.bit_length() - 1
-        )
-        spread = slot_of == lax.broadcasted_iota(jnp.int32, (count, far_rows), 0)
-        onehot[...] = jnp.dot(
-            chosen.astype(jnp.float32).astype(jnp.bfloat16),
-            spread.astype(jnp.float32).astype(jnp.bfloat16),
-            preferred_element_type=jnp.float32,
-        )
+        tile_of = lax.broadcasted_iota(jnp.int32, (tiles, n), 0)
+        block_of = lax.shift_right_logical(
+            lax.broadcasted_iota(jnp.int32, (n, far_rows), 1), blk.bit_length() - 1
+        )
+        peer_of = lax.broadcasted_iota(jnp.int32, (n, far_rows), 0)
+        table = jnp.zeros((tiles, far_rows), jnp.float32)
+        for k in range(slots):
+            target = jnp.where(count_ref[...] > k, tile_ref[k : k + 1, :], -1)
+            chosen = (tile_of == target).astype(jnp.float32)
+            spread = (block_of == peer_of * slots + k).astype(jnp.float32)
+            table = table + jnp.dot(
+                chosen.astype(jnp.bfloat16),
+                spread.astype(jnp.bfloat16),
+                preferred_element_type=jnp.float32,
+            )
+        onehot[...] = table
 
         @pl.loop(0, tiles)
         def _(t):
@@ -218,45 +227,60 @@
             out_sem,
         )
 
+    pairs = tiles // 2
+    copies = halo_first
     for it in range(ITERS):
-        if it:
-            copies = halo_copies(
-                it, cur[it].at[groups(tile, tile)], cur[it].at[groups(rows, tile)]
-            )
-        else:
-            copies = halo_first
         exchange(it)
-        if it:
-            for copy in copies:
-                copy.start()
-        else:
+        if it == 0:
             farw_copy.wait()
             band_copy.wait()
             prepare()
+        band_pass(it, 1, pairs - 1)
         await_halo(it, copies)
-        band_pass(it)
+        band_pass(it, 0, 1)
+        band_pass(it, pairs - 1, pairs)
         await_blocks(it)
 
         last = it == ITERS - 1
-
-        @pl.loop(0, tiles // 2)
-        def _(p):
-            far_pass(it, p)
-            finish(it, p)
+        if not last:
+            copies = halo_copies(
+                it + 1, cur[it + 1].at[groups(tile, tile)], cur[it + 1].at[groups(rows, tile)]
+            )
+
+        def pair_at(i):
+            return lax.rem(i + pairs - 1, pairs)
+
+        far_pass(it, pair_at(0), far_a)
+
+        @pl.loop(0, pairs // 2)
+        def _(q):
+            far_pass(it, pair_at(2 * q + 1), far_b)
+            finish(it, pair_at(2 * q), far_a)
+            far_pass(it, pair_at(2 * q + 2), far_a)
+            finish(it, pair_at(2 * q + 1), far_b)
             if last:
 
-                @pl.when(p > 0)
+                @pl.when(q > 0)
                 def _():
-                    out_copy(p - 1).start()
+                    out_copy(pair_at(2 * q - 2)).start()
+                    out_copy(pair_at(2 * q - 1)).start()
+
+            else:
+
+                @pl.when(q == 1)
+                def _():
+                    for copy in copies:
+                        copy.start()
 
         sums = jnp.sum(part[...], axis=1)
         res_ref[it : it + 1, :] = jnp.sum(sums.T, axis=0, keepdims=True)
 
-    out_copy(tiles // 2 - 1).start()
+    out_copy(pairs - 3).start()
+    out_copy(pairs - 2).start()
     whole = pltpu.make_async_copy(cur[ITERS % 2].at[groups(tile, rows)], out_hbm, out_sem)
     whole.wait()
     both = pl.ds(0, n - 1)
-    pltpu.make_async_copy(req_ref.at[both], req_ref.at[both], req_send).wait()
+    pltpu.make_async_copy(req_in.at[both], req_in.at[both], req_send).wait()
 
 
 def body(labels, seed_mask, band_w, far_block, far_tile, far_count, far_w):
@@ -265,9 +289,6 @@
     _, n, slots, blk, _ = far_w.shape
     lane = 128
     per = slots * blk
-    live = jnp.arange(slots, dtype=jnp.int32)[None, :] < far_count[0][:, None]
-    slot_tile = jnp.where(live, far_tile[0], -1).reshape(1, n * slots)
-    requests = jnp.pad(far_block[0], ((0, 0), (0, lane - slots))).reshape(n, 1, lane)
     dims = (n, tiles, tile, slots, blk, classes)
     vmem, anywhere = pltpu.VMEM, pl.BlockSpec(memory_space=pl.ANY)
     held = pl.BlockSpec(memory_space=pltpu.VMEM)
@@ -279,7 +300,7 @@
             jax.ShapeDtypeStruct((rows // GROUP, GROUP, classes), bf16),
             jax.ShapeDtypeStruct((ITERS, tiles), f32),
         ),
-        in_specs=[anywhere, anywhere, anywhere, held, held, held],
+        in_specs=[anywhere, anywhere, anywhere, held, held, held, held],
         out_specs=(anywhere, held),
         scratch_shapes=[
             vmem(((rows + 2 * tile) // GROUP, GROUP, classes), bf16),
@@ -290,6 +311,8 @@
             vmem((tiles, n * per), f32),
             vmem((rows, n * per), bf16),
             vmem((rows, classes), f32),
+            vmem((2 * tile, classes), f32),
+            vmem((2 * tile, classes), f32),
             vmem((rows, lane), f32),
             vmem((tiles, 8, lane), f32),
             vmem((2, tile // GROUP, GROUP, classes), bf16),
@@ -298,8 +321,8 @@
             vmem((n, per, classes), bf16),
             vmem((n, per, classes), bf16),
             vmem((n, per, classes), bf16),
-            vmem((n, 1, lane), jnp.int32),
-            pltpu.SMEM((n, 1, lane), jnp.int32),
+            vmem((n, slots, n), jnp.int32),
+            pltpu.SMEM((n, slots, n), jnp.int32),
             dma, dma, dma, dma, dma,
             dma, dma,
             dma((ITERS, 2)), dma((ITERS, 2)),
@@ -312,8 +335,9 @@
         labels.reshape(rows // GROUP, GROUP, classes),
         band_w,
         far_w.reshape(n * per, tile),
-        requests,
-        slot_tile,
+        far_block[0].T,
+        far_tile[0].T,
+        far_count,
         seed_mask.reshape(tiles, tile),
     )
     return out.reshape(rows, classes), residual

time: 74.5 us -> 57.9 us (0.78)
  the two profiles are of different devices: /device:TPU:0 before, /device:TPU:29 now
where the time goes in v2:
time: 57.9 us; the launch traced here: 57.7 us
  Pallas kernels  52 us (90%)
  local copies, waits for them, and re-layouts  5.04 us (9%)
  between operations  0.65 us (1%)
    pallas_call x1, Pallas kernels, body(): pl.pallas_call(functools.partial(kernel, dims), out_shape=(jax.ShapeDtype...  52 us
    unnamed x4, local copies, waits for them, and re-layouts  5.04 us

profile of v2, /device:TPU:29, one launch (start us, length us, event | category | flops | bytes accessed | tf_op | source)
XLA Modules:
  0.0 57.7 jit_solution(12732091222245085051)
XLA Ops:
  0.6 52.0 %shard_map.86 = (bf16[256,16,512]{2,1,0:T(8,128)(2,1)}, f32[2,32]{1,0:T(2,128)}) custom-call(bf16[256,16,512]{2,1,0:T(8,128)(2,1)} %bitcast.10, bf16[32,3,128,128]{3,2,1,0:T(8,128)(2,1)} %band_hbm.1, bf16[512,128]{1,0:T(8,128)(2,1)} %bitcast.12, s32[2,32]{1,0:T(2,128)} %bitcast.14, s32[2,32]{1,0:T(2,128)} %bitcast.15, s32[1,32]{1,0:T(1,128)} %count_ref.1, ...), custom_call_target="tpu_custom_call" | custom-call | tf_op jit(solution)/shard_map/pallas_call | solution.py:297
  52.6 0.0 copy-start
  52.6 4.5 %copy.11 = bf16[4096,512]{1,0:T(8,128)(2,1)} copy(bf16[4096,512]{1,0:T(8,128)(2,1)} %bitcast.11) | data formatting | bytes 8388608
  57.1 0.0 copy-done
  57.1 0.6 copy.12
Async XLA Ops:
  52.6 4.5 %copy-start = (f32[2,32]{1,0:T(2,128)S(1)}, f32[2,32]{1,0:T(2,128)}, u32[]{:S(2)}) copy-start(f32[2,32]{1,0:T(2,128)} %get-tuple-element.9) | copy-start | bytes 772

commit v3 on v2

--- a/solution.py
+++ b/solution.py
@@ -16,10 +16,10 @@
 def kernel(
     dims,
     labels_hbm, band_hbm, farw_hbm, req_ref, tile_ref, count_ref, seed_ref,
-    out_hbm, res_ref,
+    out_ref, res_ref,
     cur0, cur1, band, farw, wide_t, onehot, placed, acc, far_a, far_b, inv, part,
     halo0, halo1, send0, send1, recv0, recv1, req_in, req_s,
-    lab_sem, band_sem, farw_sem, smem_sem, out_sem,
+    lab_sem, band_sem, farw_sem, smem_sem,
     req_send, req_recv, halo_send, halo_recv, blk_send, blk_recv,
 ):
     n, tiles, tile, slots, blk, classes = dims
@@ -153,7 +153,8 @@
         )
 
     def finish(it, p, far):
-        target = cur[1 - it]
+        last = it == ITERS - 1
+        target = out_ref if last else cur[1 - it]
         for half in range(2):
             total = jnp.zeros((8, lane), jnp.float32)
             for r in range(0, tile, ROWS):
@@ -175,11 +176,12 @@
                 padded = pl.ds(
                     p * (2 * tile // GROUP) + (half * tile + r + tile) // GROUP, ROWS // GROUP
                 )
+                written = pl.ds(padded.start - tile // GROUP, padded.size) if last else padded
                 for q, s in enumerate(spread):
                     where = slice(q * lane, (q + 1) * lane)
                     before = cur[it][padded, :, where].reshape(ROWS, lane).astype(jnp.float32)
                     fresh = jnp.where(keep, before, s * factor).astype(jnp.bfloat16)
-                    target[padded, :, where] = fresh.reshape(ROWS // GROUP, GROUP, lane)
+                    target[written, :, where] = fresh.reshape(ROWS // GROUP, GROUP, lane)
                     change = jnp.abs(fresh.astype(jnp.float32) - before)
                     for i in range(0, ROWS, 8):
                         total = total + change[i : i + 8]
@@ -219,14 +221,6 @@
             inverse = jnp.broadcast_to(1.0 / degree, (tile, tile))
             inv[pl.ds(base, tile), :] = jnp.where(seeded == 1.0, -inverse, inverse)
 
-    def out_copy(p):
-        base = p * (2 * tile // GROUP)
-        return pltpu.make_async_copy(
-            cur[ITERS % 2].at[pl.ds(base + tile // GROUP, 2 * tile // GROUP)],
-            out_hbm.at[pl.ds(base, 2 * tile // GROUP)],
-            out_sem,
-        )
-
     pairs = tiles // 2
     copies = halo_first
     for it in range(ITERS):
@@ -258,14 +252,7 @@
             finish(it, pair_at(2 * q), far_a)
             far_pass(it, pair_at(2 * q + 2), far_a)
             finish(it, pair_at(2 * q + 1), far_b)
-            if last:
-
-                @pl.when(q > 0)
-                def _():
-                    out_copy(pair_at(2 * q - 2)).start()
-                    out_copy(pair_at(2 * q - 1)).start()
-
-            else:
+            if not last:
 
                 @pl.when(q == 1)
                 def _():
@@ -275,10 +262,6 @@
         sums = jnp.sum(part[...], axis=1)
         res_ref[it : it + 1, :] = jnp.sum(sums.T, axis=0, keepdims=True)
 
-    out_copy(pairs - 3).start()
-    out_copy(pairs - 2).start()
-    whole = pltpu.make_async_copy(cur[ITERS % 2].at[groups(tile, rows)], out_hbm, out_sem)
-    whole.wait()
     both = pl.ds(0, n - 1)
     pltpu.make_async_copy(req_in.at[both], req_in.at[both], req_send).wait()
 
@@ -297,11 +280,11 @@
     out, residual = pl.pallas_call(
         functools.partial(kernel, dims),
         out_shape=(
-            jax.ShapeDtypeStruct((rows // GROUP, GROUP, classes), bf16),
+            pltpu.VMEM((rows // GROUP, GROUP, classes), bf16),
             jax.ShapeDtypeStruct((ITERS, tiles), f32),
         ),
         in_specs=[anywhere, anywhere, anywhere, held, held, held, held],
-        out_specs=(anywhere, held),
+        out_specs=(held, held),
         scratch_shapes=[
             vmem(((rows + 2 * tile) // GROUP, GROUP, classes), bf16),
             vmem(((rows + 2 * tile) // GROUP, GROUP, classes), bf16),
@@ -323,13 +306,13 @@
             vmem((n, per, classes), bf16),
             vmem((n, slots, n), jnp.int32),
             pltpu.SMEM((n, slots, n), jnp.int32),
-            dma, dma, dma, dma, dma,
+            dma, dma, dma, dma,
             dma, dma,
             dma((ITERS, 2)), dma((ITERS, 2)),
             dma((ITERS,)), dma((ITERS,)),
         ],
         compiler_params=pltpu.CompilerParams(
-            collective_id=0, has_side_effects=True, vmem_limit_bytes=60 * 1024 * 1024
+            collective_id=0, has_side_effects=True, vmem_limit_bytes=56 * 1024 * 1024
         ),
     )(
         labels.reshape(rows // GROUP, GROUP, classes),

time: 57.9 us -> 54.7 us (0.945)
  local copies, waits for them, and re-layouts: 5.04 us -> 2.58 us
  Pallas kernels: 52 us -> 51.2 us
    unnamed x4, local copies, waits for them, and re-layouts: 5.04 us -> 2.58 us
    pallas_call x1, Pallas kernels: 52 us -> 51.2 us  [body(): pl.pallas_call(functools.partial(kernel, dims), out_shape=(pltpu.VMEM((ro...]
where the time goes in v3:
time: 54.7 us; the launch traced here: 54.4 us
  Pallas kernels  51.2 us (94%)
  local copies, waits for them, and re-layouts  2.58 us (5%)
  between operations  0.65 us (1%)
    pallas_call x1, Pallas kernels, body(): pl.pallas_call(functools.partial(kernel, dims), out_shape=(pltpu.VMEM((ro...  51.2 us
    unnamed x4, local copies, waits for them, and re-layouts  2.58 us

profile of v3, /device:TPU:29, one launch (start us, length us, event | category | flops | bytes accessed | tf_op | source)
XLA Modules:
  0.0 54.4 jit_solution(17920197537995960661)
XLA Ops:
  0.6 51.2 %shard_map.86 = (bf16[256,16,512]{2,1,0:T(8,128)(2,1)S(1)}, f32[2,32]{1,0:T(2,128)}) custom-call(bf16[256,16,512]{2,1,0:T(8,128)(2,1)} %bitcast.11, bf16[32,3,128,128]{3,2,1,0:T(8,128)(2,1)} %band_hbm.1, bf16[512,128]{1,0:T(8,128)(2,1)} %bitcast.12, s32[2,32]{1,0:T(2,128)} %bitcast.14, s32[2,32]{1,0:T(2,128)} %bitcast.15, s32[1,32]{1,0:T(1,128)} %count_ref.1, ...), custom_call_target="tpu_custom_call" | custom-call | tf_op jit(solution)/shard_map/pallas_call | solution.py:280
  51.8 0.0 copy-start
  51.8 2.0 %copy.11 = bf16[4096,512]{1,0:T(8,128)(2,1)} copy(bf16[4096,512]{1,0:T(8,128)(2,1)S(1)} %bitcast.10) | data formatting | bytes 8388608
  53.9 0.0 copy-done
  53.9 0.6 %copy.12 = f32[2,32]{1,0:T(2,128)} copy(f32[2,32]{1,0:T(2,128)S(1)} %copy-done) | data formatting | bytes 512
Async XLA Ops:
  51.8 2.0 %copy-start = (f32[2,32]{1,0:T(2,128)S(1)}, f32[2,32]{1,0:T(2,128)}, u32[]{:S(2)}) copy-start(f32[2,32]{1,0:T(2,128)} %get-tuple-element.11) | copy-start | bytes 772
